TPU v7x, 256 devices: a whole 4x4x8 slice. The times are simulated.
256 devices in a mesh: lat: 4 (over y), lon: 64 (over x, z, core).
Axes of the slice: x: 4, y: 4, z: 8, core: 2. Of those that a mesh axis runs over, the one named last changes fastest.
Arguments:
- right_side: float32 [512, 8192], P('lat', 'lon'), may hold values from -8 to 8
- surface_term: float32 [512, 8192], P('lat', 'lon'), may hold values from 0.0002 to 0.002
- east_coupling: float32 [512, 8192], P('lat', 'lon'), may hold values from 0.3 to 3
- north_coupling: float32 [512, 8192], P('lat', 'lon'), may hold values from 0.3 to 3
- neast_coupling: float32 [512, 8192], P('lat', 'lon'), may hold values from 0.1 to 0.5
- nwest_coupling: float32 [512, 8192], P('lat', 'lon'), may hold values from 0.1 to 0.5
- land_sea: int32 [512, 8192], P('lat', 'lon'), may hold values from 0 to 1, as said below
- fold_map: int32 [8192], P('lon'), may hold values from 0 to 8191, as said below
Outputs:
- solution: float32 [512, 8192], P('lat', 'lon')
- residual: float32 [512, 8192], P('lat', 'lon')
Inputs may be any that keep to these rules, and one draw needn't show every extreme that they name: fold_map[j] = (c - j) mod 8192 for one odd c: an involution of the columns with no fixed point. land_sea is 0 or 1; land lies in bands of 8 columns, each over one range of rows.
All inputs are finite; a program needn't handle non-finite values.
Results may differ from a plain program's by a relative error of at most 0.0015.
Values sent between devices are 32-bit elements.
No kernel may reach another device: no remote copies, remote signals or barrier semaphores. Data moves between devices by JAX's collectives and lax.ppermute only.
A program may use at most 64 MiB of HBM per device.

v0:
```python
import functools

import jax
import jax.numpy as jnp
from jax import lax
from jax.sharding import Mesh
from jax.sharding import PartitionSpec as P

ITERS = 8
LAT_LON = ("lat", "lon_0", "lon_1", "lon_2")
LON = ("lon_0", "lon_1", "lon_2")


OFFSETS = ((0, 1), (0, -1), (1, 0), (-1, 0), (1, 1), (-1, -1), (1, -1), (-1, 1))
COUPLINGS = (
    (1, 0, 0),
    (1, 0, -1),
    (2, 0, 0),
    (2, -1, 0),
    (3, 0, 0),
    (3, -1, -1),
    (4, 0, 0),
    (4, -1, 1),
)


def one_axis_at_a_time(shard, axes):
    return functools.reduce(lax.psum, axes, shard)


def with_halo(shard, sides, width):
    for axis, dim in sides:
        size, length = (lax.axis_size(axis), shard.shape[dim])
        up = [(i, (i + 1) % size) for i in range(size)]
        down = [(j, i) for i, j in up]
        last = lax.slice_in_dim(shard, length - width, length, axis=dim)
        first = lax.slice_in_dim(shard, 0, width, axis=dim)
        before = lax.ppermute(last, axis, up)
        after = lax.ppermute(first, axis, down)
        shard = jnp.concatenate([before, shard, after], axis=dim)
    return shard


def joined_along(blocks, dim):
    blocks = jnp.moveaxis(blocks, 0, dim)
    shape = blocks.shape
    return blocks.reshape(*shape[:dim], shape[dim] * shape[dim + 1], *shape[dim + 2 :])


def copy_for_each(shard, axis):
    copies = jnp.broadcast_to(shard, (lax.axis_size(axis), *shard.shape))
    return lax.all_to_all(copies, axis, split_axis=0, concat_axis=0, tiled=True)


def gathered_copies(shard, axis, dim):
    return joined_along(copy_for_each(shard, axis), dim)


def interior(padded, row_step, col_step):
    row_count = padded.shape[-2] - 2
    col_count = padded.shape[-1] - 2
    return padded[
        ..., 1 + row_step : 1 + row_step + row_count, 1 + col_step : 1 + col_step + col_count
    ]


def stencil_weights(padded):
    ocean_pad = padded[0]
    centre = interior(ocean_pad, 0, 0)
    weight_list = []
    open_sum = jnp.zeros_like(centre)
    for (layer_index, row_step, col_step), (row_off, col_off) in zip(COUPLINGS, OFFSETS):
        edge_value = interior(padded[layer_index], row_step, col_step)
        weight_list.append(edge_value * centre * interior(ocean_pad, row_off, col_off))
        open_sum = open_sum + edge_value
    return (jnp.stack(weight_list), open_sum)


def neighbour_sum(weights, padded_field):
    accumulated = jnp.zeros_like(weights[0])
    for position, (row_off, col_off) in enumerate(OFFSETS):
        accumulated = accumulated + weights[position] * interior(padded_field, row_off, col_off)
    return accumulated


def shift_down(values, stride, fill):
    pad_shape = values.shape[:-2] + (stride, values.shape[-1])
    filler = jnp.full(pad_shape, fill, values.dtype)
    return jnp.concatenate([filler, values[..., :-stride, :]], axis=-2)


def shift_up(values, stride, fill):
    pad_shape = values.shape[:-2] + (stride, values.shape[-1])
    filler = jnp.full(pad_shape, fill, values.dtype)
    return jnp.concatenate([values[..., stride:, :], filler], axis=-2)


def reduction_plan(lower_band, middle_band, upper_band):
    factors = []
    stride = 1
    while stride < middle_band.shape[-2]:
        left_factor = lower_band / shift_down(middle_band, stride, 1.0)
        right_factor = upper_band / shift_up(middle_band, stride, 1.0)
        new_middle = (
            middle_band
            - shift_down(upper_band, stride, 0.0) * left_factor
            - shift_up(lower_band, stride, 0.0) * right_factor
        )
        lower_band = -shift_down(lower_band, stride, 0.0) * left_factor
        upper_band = -shift_up(upper_band, stride, 0.0) * right_factor
        middle_band = new_middle
        factors.append((left_factor, right_factor))
        stride = stride * 2
    return (factors, middle_band)


def reduce_apply(factors, pivots, values):
    stride = 1
    for left_factor, right_factor in factors:
        values = (
            values
            - left_factor * shift_down(values, stride, 0.0)
            - right_factor * shift_up(values, stride, 0.0)
        )
        stride = stride * 2
    return values / pivots


def reduced_inverse(all_responses, lat_count):
    order_count = 2 * lat_count
    col_count = all_responses.shape[-1]
    identity = jnp.broadcast_to(
        jnp.eye(order_count, dtype=jnp.float32)[:, :, None], (order_count, order_count, col_count)
    )
    matrix = identity
    for block_index in range(lat_count):
        if block_index > 0:
            matrix = matrix.at[2 * block_index, 2 * block_index - 1].set(
                -all_responses[4 * block_index]
            )
            matrix = matrix.at[2 * block_index + 1, 2 * block_index - 1].set(
                -all_responses[4 * block_index + 1]
            )
        if block_index < lat_count - 1:
            matrix = matrix.at[2 * block_index, 2 * block_index + 2].set(
                -all_responses[4 * block_index + 2]
            )
            matrix = matrix.at[2 * block_index + 1, 2 * block_index + 2].set(
                -all_responses[4 * block_index + 3]
            )
    inverse = identity
    for pivot_row in range(order_count):
        pivot_value = matrix[pivot_row, pivot_row]
        scaled_matrix = matrix[pivot_row] / pivot_value
        scaled_inverse = inverse[pivot_row] / pivot_value
        pivot_column = matrix[:, pivot_row]
        matrix = matrix - pivot_column[:, None] * scaled_matrix[None]
        inverse = inverse - pivot_column[:, None] * scaled_inverse[None]
        matrix = matrix.at[pivot_row].set(scaled_matrix)
        inverse = inverse.at[pivot_row].set(scaled_inverse)
    return inverse


def both_products(residual, precond, image_field):
    return (
        one_axis_at_a_time(jnp.sum(residual * precond), LAT_LON),
        one_axis_at_a_time(jnp.sum(image_field * precond), LAT_LON),
    )


def shards(
    right_side,
    surface_term,
    east_coupling,
    north_coupling,
    neast_coupling,
    nwest_coupling,
    land_sea,
    fold_map,
):
    row_count, col_count = right_side.shape
    lat_count = lax.axis_size("lat")
    lat_place = lax.axis_index("lat")
    is_top = (lat_place == lat_count - 1).astype(jnp.float32)
    is_bottom = (lat_place == 0).astype(jnp.float32)
    ocean = land_sea.astype(jnp.float32)
    row_ids = lax.broadcasted_iota(jnp.int32, (row_count, col_count), 0)
    top_row = jnp.where(row_ids == row_count - 1, is_top, 0.0)
    open_rows = 1.0 - top_row
    stacked = jnp.stack(
        [
            ocean,
            east_coupling,
            north_coupling * open_rows,
            neast_coupling * open_rows,
            nwest_coupling * open_rows,
        ]
    )
    padded = with_halo(stacked, (("lat", 1), (LON, 2)), 1)
    pad_rows = lax.broadcasted_iota(jnp.int32, (row_count + 2, 1), 0)
    closed = (pad_rows == 0) & (lat_place == 0) | (pad_rows == row_count + 1) & (
        lat_place == lat_count - 1
    )
    padded = jnp.where(closed[None], 0.0, padded)
    weights, open_sum = stencil_weights(padded)
    top_pair = jnp.stack([north_coupling[-1], ocean[-1]])
    whole_top = gathered_copies(top_pair, LON, 1)
    partner = jnp.take(whole_top, fold_map, axis=1)
    fold_open = 0.5 * (north_coupling[-1] + partner[0]) * is_top
    fold_weight = fold_open * ocean[-1] * partner[1]
    diagonal = ocean * (surface_term + open_sum + top_row * fold_open[None]) + (1.0 - ocean)
    line_diagonal = ocean * (surface_term + weights[2] + weights[3]) + (1.0 - ocean)

    def operate(field, south_row, north_row):
        extended = jnp.concatenate([south_row[None], field, north_row[None]], axis=0)
        padded_field = with_halo(extended, ((LON, 1),), 1)
        whole_row = gathered_copies(field[-1], LON, 0)
        fold_term = fold_weight * jnp.take(whole_row, fold_map)
        return diagonal * field - neighbour_sum(weights, padded_field) - top_row * fold_term[None]

    local_lower = jnp.where(row_ids > 0, -weights[3], 0.0)
    local_upper = jnp.where(row_ids < row_count - 1, -weights[2], 0.0)
    factors, pivots = reduction_plan(local_lower, line_diagonal, local_upper)
    boundary = jnp.stack(
        [
            jnp.where(row_ids == 0, weights[3], 0.0),
            jnp.where(row_ids == row_count - 1, weights[2], 0.0),
        ]
    )
    responses = reduce_apply(factors, pivots, boundary)
    response_ends = jnp.stack(
        [responses[0, 0], responses[0, -1], responses[1, 0], responses[1, -1]]
    )
    all_responses = gathered_copies(response_ends, "lat", 0)
    coupling_inverse = reduced_inverse(all_responses, lat_count)
    below_index = jnp.maximum(2 * lat_place - 1, 0)
    above_index = jnp.minimum(2 * lat_place + 2, 2 * lat_count - 1)

    def precondition(residual_now):
        local_part = reduce_apply(factors, pivots, residual_now)
        end_values = jnp.stack([local_part[0], local_part[-1]])
        gathered_ends = lax.all_gather(end_values, "lat", axis=0, tiled=True)
        boundary_values = jnp.sum(coupling_inverse * gathered_ends[None], axis=1)
        below_value = lax.dynamic_index_in_dim(boundary_values, below_index, 0, keepdims=False)
        above_value = lax.dynamic_index_in_dim(boundary_values, above_index, 0, keepdims=False)
        result = local_part + below_value[None] * responses[0] + above_value[None] * responses[1]
        return (result, below_value * (1.0 - is_bottom), above_value * (1.0 - is_top))

    residual = ocean * right_side
    precond, south_now, north_now = precondition(residual)
    image_field = operate(precond, south_now, north_now)
    product_now, curvature = both_products(residual, precond, image_field)
    step_length = product_now / curvature
    direction = precond
    along_field = image_field
    solution = step_length * direction
    residual = residual - step_length * along_field
    for iteration in range(1, ITERS):
        precond, south_now, north_now = precondition(residual)
        image_field = operate(precond, south_now, north_now)
        product_next, curvature = both_products(residual, precond, image_field)
        ratio_next = product_next / product_now
        step_length = product_next / (curvature - ratio_next * product_next / step_length)
        direction = precond + ratio_next * direction
        along_field = image_field + ratio_next * along_field
        solution = solution + step_length * direction
        residual = residual - step_length * along_field
        product_now = product_next
    return (solution, residual)


def solution(mesh):
    finer = Mesh(
        mesh.devices.reshape(mesh.shape["lat"], 4, 8, 2), ("lat", "lon_0", "lon_1", "lon_2")
    )
    placed = (
        P("lat", LON),
        P("lat", LON),
        P("lat", LON),
        P("lat", LON),
        P("lat", LON),
        P("lat", LON),
        P("lat", LON),
        P(LON),
    )
    return jax.shard_map(
        shards,
        mesh=finer,
        in_specs=placed,
        out_specs=(P("lat", LON), P("lat", LON)),
        check_vma=False,
    )
```

profile of v0, /device:TPU:1, one launch (start us, length us, event | category | flops | bytes accessed | tf_op | source)
XLA Modules:
  0.0 649.1 jit_solution(12013515594875392302)
XLA Ops:
  50.9 12.0 %all-to-all-start.2 = ((f32[64,1,128]{2,1,0:T(1,128)}), f32[64,1,128]{2,1,0:T(1,128)S(1)}, u32[]{:S(2)}, u32[]{:S(2)}) async-start(f32[64,1,128]{2,1,0:T(1,128)} %broadcast_in_dim.94), calls=%async_computation.2 | async-start | bytes 65536 | tf_op jit(solution)/shard_map/all_to_all | solution.py:52
  109.5 11.9 %all-reduce.173 = (f32[]{:T(128)}, f32[]{:T(128)}) all-reduce(f32[]{:T(128)} %get-tuple-element.385, f32[]{:T(128)} %get-tuple-element.386), channel_id=1, replica_groups=mesh['lat'=4,'lon_0'=4,'lon_1'=8,'lon_2'=2] {'lon_1'}, use_global_device_ids=true, to_apply=%region_5.6 | all-reduce | flops 2 | bytes 16 | tf_op jit(solution)/shard_map/psum | solution.py:28
  121.3 10.5 %all-reduce.197 = (f32[]{:T(128)}, f32[]{:T(128)}) all-reduce(f32[]{:T(128)} %get-tuple-element.369, f32[]{:T(128)} %get-tuple-element.370), channel_id=1, replica_groups=mesh['lat'=4,'lon_0'=4,'lon_1'=8,'lon_2'=2] {'lon_2'}, use_global_device_ids=true, to_apply=%region_6.7 | all-reduce | flops 2 | bytes 16 | tf_op jit(solution)/shard_map/psum | solution.py:28
  154.6 9.2 %all-to-all-done.3 = f32[64,1,128]{2,1,0:T(1,128)S(1)} async-done(((f32[64,1,128]{2,1,0:T(1,128)}), f32[64,1,128]{2,1,0:T(1,128)S(1)}, u32[]{:S(2)}, u32[]{:S(2)}) %all-to-all-start.3) | async-done | bytes 32800 | tf_op jit(solution)/shard_map/all_to_all | solution.py:52
  179.9 11.7 %all-reduce.172 = (f32[]{:T(128)}, f32[]{:T(128)}) all-reduce(f32[]{:T(128)} %get-tuple-element.383, f32[]{:T(128)} %get-tuple-element.384), channel_id=1, replica_groups=mesh['lat'=4,'lon_0'=4,'lon_1'=8,'lon_2'=2] {'lon_1'}, use_global_device_ids=true, to_apply=%region_16.18 | all-reduce | flops 2 | bytes 16 | tf_op jit(solution)/shard_map/psum | solution.py:28
  191.6 11.0 %all-reduce.196 = (f32[]{:T(128)}, f32[]{:T(128)}) all-reduce(f32[]{:T(128)} %get-tuple-element.367, f32[]{:T(128)} %get-tuple-element.368), channel_id=1, replica_groups=mesh['lat'=4,'lon_0'=4,'lon_1'=8,'lon_2'=2] {'lon_2'}, use_global_device_ids=true, to_apply=%region_17.19 | all-reduce | flops 2 | bytes 16 | tf_op jit(solution)/shard_map/psum | solution.py:28
  228.8 9.2 %all-to-all-done.4 = f32[64,1,128]{2,1,0:T(1,128)S(1)} async-done(((f32[64,1,128]{2,1,0:T(1,128)}), f32[64,1,128]{2,1,0:T(1,128)S(1)}, u32[]{:S(2)}, u32[]{:S(2)}) %all-to-all-start.4) | async-done | bytes 32800 | tf_op jit(solution)/shard_map/all_to_all | solution.py:52
  253.9 11.6 %all-reduce.171 = (f32[]{:T(128)}, f32[]{:T(128)}) all-reduce(f32[]{:T(128)} %get-tuple-element.381, f32[]{:T(128)} %get-tuple-element.382), channel_id=1, replica_groups=mesh['lat'=4,'lon_0'=4,'lon_1'=8,'lon_2'=2] {'lon_1'}, use_global_device_ids=true, to_apply=%region_27.29 | all-reduce | flops 2 | bytes 16 | tf_op jit(solution)/shard_map/psum | solution.py:28
  265.6 10.9 %all-reduce.195 = (f32[]{:T(128)}, f32[]{:T(128)}) all-reduce(f32[]{:T(128)} %get-tuple-element.365, f32[]{:T(128)} %get-tuple-element.366), channel_id=1, replica_groups=mesh['lat'=4,'lon_0'=4,'lon_1'=8,'lon_2'=2] {'lon_2'}, use_global_device_ids=true, to_apply=%region_28.30 | all-reduce | flops 2 | bytes 16 | tf_op jit(solution)/shard_map/psum | solution.py:28
  302.3 9.2 %all-to-all-done.5 = f32[64,1,128]{2,1,0:T(1,128)S(1)} async-done(((f32[64,1,128]{2,1,0:T(1,128)}), f32[64,1,128]{2,1,0:T(1,128)S(1)}, u32[]{:S(2)}, u32[]{:S(2)}) %all-to-all-start.5) | async-done | bytes 32800 | tf_op jit(solution)/shard_map/all_to_all | solution.py:52
  327.5 11.7 %all-reduce.170 = (f32[]{:T(128)}, f32[]{:T(128)}) all-reduce(f32[]{:T(128)} %get-tuple-element.379, f32[]{:T(128)} %get-tuple-element.380), channel_id=1, replica_groups=mesh['lat'=4,'lon_0'=4,'lon_1'=8,'lon_2'=2] {'lon_1'}, use_global_device_ids=true, to_apply=%region_38.40 | all-reduce | flops 2 | bytes 16 | tf_op jit(solution)/shard_map/psum | solution.py:28
  339.2 10.9 %all-reduce.194 = (f32[]{:T(128)}, f32[]{:T(128)}) all-reduce(f32[]{:T(128)} %get-tuple-element.363, f32[]{:T(128)} %get-tuple-element.364), channel_id=1, replica_groups=mesh['lat'=4,'lon_0'=4,'lon_1'=8,'lon_2'=2] {'lon_2'}, use_global_device_ids=true, to_apply=%region_39.41 | all-reduce | flops 2 | bytes 16 | tf_op jit(solution)/shard_map/psum | solution.py:28
  375.5 9.2 %all-to-all-done.6 = f32[64,1,128]{2,1,0:T(1,128)S(1)} async-done(((f32[64,1,128]{2,1,0:T(1,128)}), f32[64,1,128]{2,1,0:T(1,128)S(1)}, u32[]{:S(2)}, u32[]{:S(2)}) %all-to-all-start.6) | async-done | bytes 32800 | tf_op jit(solution)/shard_map/all_to_all | solution.py:52
  400.6 11.6 %all-reduce.169 = (f32[]{:T(128)}, f32[]{:T(128)}) all-reduce(f32[]{:T(128)} %get-tuple-element.377, f32[]{:T(128)} %get-tuple-element.378), channel_id=1, replica_groups=mesh['lat'=4,'lon_0'=4,'lon_1'=8,'lon_2'=2] {'lon_1'}, use_global_device_ids=true, to_apply=%region_49.51 | all-reduce | flops 2 | bytes 16 | tf_op jit(solution)/shard_map/psum | solution.py:28
  412.3 11.0 %all-reduce.193 = (f32[]{:T(128)}, f32[]{:T(128)}) all-reduce(f32[]{:T(128)} %get-tuple-element.361, f32[]{:T(128)} %get-tuple-element.362), channel_id=1, replica_groups=mesh['lat'=4,'lon_0'=4,'lon_1'=8,'lon_2'=2] {'lon_2'}, use_global_device_ids=true, to_apply=%region_50.52 | all-reduce | flops 2 | bytes 16 | tf_op jit(solution)/shard_map/psum | solution.py:28
  448.6 9.2 %all-to-all-done.7 = f32[64,1,128]{2,1,0:T(1,128)S(1)} async-done(((f32[64,1,128]{2,1,0:T(1,128)}), f32[64,1,128]{2,1,0:T(1,128)S(1)}, u32[]{:S(2)}, u32[]{:S(2)}) %all-to-all-start.7) | async-done | bytes 32800 | tf_op jit(solution)/shard_map/all_to_all | solution.py:52
  473.9 11.7 %all-reduce.168 = (f32[]{:T(128)}, f32[]{:T(128)}) all-reduce(f32[]{:T(128)} %get-tuple-element.375, f32[]{:T(128)} %get-tuple-element.376), channel_id=1, replica_groups=mesh['lat'=4,'lon_0'=4,'lon_1'=8,'lon_2'=2] {'lon_1'}, use_global_device_ids=true, to_apply=%region_60.62 | all-reduce | flops 2 | bytes 16 | tf_op jit(solution)/shard_map/psum | solution.py:28
  485.6 11.2 %all-reduce.192 = (f32[]{:T(128)}, f32[]{:T(128)}) all-reduce(f32[]{:T(128)} %get-tuple-element.359, f32[]{:T(128)} %get-tuple-element.360), channel_id=1, replica_groups=mesh['lat'=4,'lon_0'=4,'lon_1'=8,'lon_2'=2] {'lon_2'}, use_global_device_ids=true, to_apply=%region_61.63 | all-reduce | flops 2 | bytes 16 | tf_op jit(solution)/shard_map/psum | solution.py:28
  522.1 9.2 %all-to-all-done.8 = f32[64,1,128]{2,1,0:T(1,128)S(1)} async-done(((f32[64,1,128]{2,1,0:T(1,128)}), f32[64,1,128]{2,1,0:T(1,128)S(1)}, u32[]{:S(2)}, u32[]{:S(2)}) %all-to-all-start.8) | async-done | bytes 32800 | tf_op jit(solution)/shard_map/all_to_all | solution.py:52
  547.3 11.6 %all-reduce.167 = (f32[]{:T(128)}, f32[]{:T(128)}) all-reduce(f32[]{:T(128)} %get-tuple-element.373, f32[]{:T(128)} %get-tuple-element.374), channel_id=1, replica_groups=mesh['lat'=4,'lon_0'=4,'lon_1'=8,'lon_2'=2] {'lon_1'}, use_global_device_ids=true, to_apply=%region_71.73 | all-reduce | flops 2 | bytes 16 | tf_op jit(solution)/shard_map/psum | solution.py:28
  558.9 11.0 %all-reduce.191 = (f32[]{:T(128)}, f32[]{:T(128)}) all-reduce(f32[]{:T(128)} %get-tuple-element.357, f32[]{:T(128)} %get-tuple-element.358), channel_id=1, replica_groups=mesh['lat'=4,'lon_0'=4,'lon_1'=8,'lon_2'=2] {'lon_2'}, use_global_device_ids=true, to_apply=%region_72.74 | all-reduce | flops 2 | bytes 16 | tf_op jit(solution)/shard_map/psum | solution.py:28
  595.3 9.2 %all-to-all-done.9 = f32[64,1,128]{2,1,0:T(1,128)S(1)} async-done(((f32[64,1,128]{2,1,0:T(1,128)}), f32[64,1,128]{2,1,0:T(1,128)S(1)}, u32[]{:S(2)}, u32[]{:S(2)}) %all-to-all-start.9) | async-done | bytes 32800 | tf_op jit(solution)/shard_map/all_to_all | solution.py:52
  620.5 11.7 %all-reduce.166 = (f32[]{:T(128)}, f32[]{:T(128)}) all-reduce(f32[]{:T(128)} %get-tuple-element.371, f32[]{:T(128)} %get-tuple-element.372), channel_id=1, replica_groups=mesh['lat'=4,'lon_0'=4,'lon_1'=8,'lon_2'=2] {'lon_1'}, use_global_device_ids=true, to_apply=%region_82.84 | all-reduce | flops 2 | bytes 16 | tf_op jit(solution)/shard_map/psum | solution.py:28
  632.2 11.0 %all-reduce.190 = (f32[]{:T(128)}, f32[]{:T(128)}) all-reduce(f32[]{:T(128)} %get-tuple-element.355, f32[]{:T(128)} %get-tuple-element.356), channel_id=1, replica_groups=mesh['lat'=4,'lon_0'=4,'lon_1'=8,'lon_2'=2] {'lon_2'}, use_global_device_ids=true, to_apply=%region_83.85 | all-reduce | flops 2 | bytes 16 | tf_op jit(solution)/shard_map/psum | solution.py:28
  (490 shorter events, 359.3 us)
Async XLA Ops:
  5.6 10.0 %collective-permute-start.1 = (f32[5,1,128]{1,2,0:T(8,128)S(1)}, f32[5,1,128]{1,2,0:T(8,128)S(1)}, u32[]{:S(2)}, u32[]{:S(2)}) collective-permute-start(f32[5,1,128]{1,2,0:T(8,128)S(1)} %get-tuple-element.486), channel_id=1, source_target_pairs={{64,0},{128,64},{192,128},{0,192},{65,1},{129,65},{193,129},{1,193... | collective-permute-start | bytes 7688 | tf_op jit(solution)/shard_map/ppermute | solution.py:39
  9.2 9.5 %collective-permute-start = (f32[5,1,128]{1,2,0:T(8,128)S(1)}, f32[5,1,128]{1,2,0:T(8,128)S(1)}, u32[]{:S(2)}, u32[]{:S(2)}) collective-permute-start(f32[5,1,128]{1,2,0:T(8,128)S(1)} %get-tuple-element.485), channel_id=1, source_target_pairs={{0,64},{64,128},{128,192},{192,0},{1,65},{65,129},{129,193},{193,1... | collective-permute-start | bytes 7688 | tf_op jit(solution)/shard_map/ppermute | solution.py:38
  34.5 11.4 %all-to-all-start = ((f32[4,4,128]{2,1,0:T(4,128)}), f32[4,4,128]{2,1,0:T(4,128)S(1)}, u32[]{:S(2)}, u32[]{:S(2)}) async-start(f32[4,4,128]{2,1,0:T(4,128)} %broadcast_in_dim.85), calls=%async_computation | async-start | bytes 16384 | tf_op jit(solution)/shard_map/all_to_all | solution.py:52
  50.9 21.4 %all-to-all-start.2 = ((f32[64,1,128]{2,1,0:T(1,128)}), f32[64,1,128]{2,1,0:T(1,128)S(1)}, u32[]{:S(2)}, u32[]{:S(2)}) async-start(f32[64,1,128]{2,1,0:T(1,128)} %broadcast_in_dim.94), calls=%async_computation.2 | async-start | bytes 65536 | tf_op jit(solution)/shard_map/all_to_all | solution.py:52
  63.1 14.9 %collective-permute-start.5 = (f32[130,1]{0,1:T(1,128)S(1)}, f32[130,1]{0,1:T(1,128)S(1)}, u32[]{:S(2)}, u32[]{:S(2)}) collective-permute-start(f32[130,1]{0,1:T(1,128)S(1)} %get-tuple-element.519), channel_id=1, source_target_pairs={{0,1},{1,2},{2,3},{3,4},{4,5},{5,6},{6,7},{7,8},{8,9},{9,10},{10,1... | collective-permute-start | bytes 1568 | tf_op jit(solution)/shard_map/ppermute | solution.py:38
  64.7 13.3 %collective-permute-start.4 = (f32[130,1]{0,1:T(1,128)S(1)}, f32[130,1]{0,1:T(1,128)S(1)}, u32[]{:S(2)}, u32[]{:S(2)}) collective-permute-start(f32[130,1]{0,1:T(1,128)S(1)} %get-tuple-element.520), channel_id=1, source_target_pairs={{1,0},{2,1},{3,2},{4,3},{5,4},{6,5},{7,6},{8,7},{9,8},{10,9},{11,1... | collective-permute-start | bytes 1568 | tf_op jit(solution)/shard_map/ppermute | solution.py:39
  72.9 14.7 %all-to-all-start.1 = ((f32[64,2,128]{2,1,0:T(2,128)}), f32[64,2,128]{2,1,0:T(2,128)S(1)}, u32[]{:S(2)}, u32[]{:S(2)}) async-start(f32[64,2,128]{2,1,0:T(2,128)} %broadcast_in_dim.91), calls=%async_computation.1 | async-start | bytes 131072 | tf_op jit(solution)/shard_map/all_to_all | solution.py:52
  142.1 12.3 %collective-permute-start.7 = (f32[130,1]{0,1:T(1,128)S(1)}, f32[130,1]{0,1:T(1,128)S(1)}, u32[]{:S(2)}, u32[]{:S(2)}) collective-permute-start(f32[130,1]{0,1:T(1,128)S(1)} %get-tuple-element.515), channel_id=1, source_target_pairs={{0,1},{1,2},{2,3},{3,4},{4,5},{5,6},{6,7},{7,8},{8,9},{9,10},{10,1... | collective-permute-start | bytes 1568 | tf_op jit(solution)/shard_map/ppermute | solution.py:38
  145.3 9.1 %collective-permute-start.6 = (f32[130,1]{0,1:T(1,128)S(1)}, f32[130,1]{0,1:T(1,128)S(1)}, u32[]{:S(2)}, u32[]{:S(2)}) collective-permute-start(f32[130,1]{0,1:T(1,128)S(1)} %get-tuple-element.516), channel_id=1, source_target_pairs={{1,0},{2,1},{3,2},{4,3},{5,4},{6,5},{7,6},{8,7},{9,8},{10,9},{11,1... | collective-permute-start | bytes 1568 | tf_op jit(solution)/shard_map/ppermute | solution.py:39
  146.2 17.6 %all-to-all-start.3 = ((f32[64,1,128]{2,1,0:T(1,128)}), f32[64,1,128]{2,1,0:T(1,128)S(1)}, u32[]{:S(2)}, u32[]{:S(2)}) async-start(f32[64,1,128]{2,1,0:T(1,128)} %broadcast_in_dim.95), calls=%async_computation.3 | async-start | bytes 65536 | tf_op jit(solution)/shard_map/all_to_all | solution.py:52
  216.3 12.3 %collective-permute-start.9 = (f32[130,1]{0,1:T(1,128)S(1)}, f32[130,1]{0,1:T(1,128)S(1)}, u32[]{:S(2)}, u32[]{:S(2)}) collective-permute-start(f32[130,1]{0,1:T(1,128)S(1)} %get-tuple-element.511), channel_id=1, source_target_pairs={{0,1},{1,2},{2,3},{3,4},{4,5},{5,6},{6,7},{7,8},{8,9},{9,10},{10,1... | collective-permute-start | bytes 1568 | tf_op jit(solution)/shard_map/ppermute | solution.py:38
  219.7 8.9 %collective-permute-start.8 = (f32[130,1]{0,1:T(1,128)S(1)}, f32[130,1]{0,1:T(1,128)S(1)}, u32[]{:S(2)}, u32[]{:S(2)}) collective-permute-start(f32[130,1]{0,1:T(1,128)S(1)} %get-tuple-element.512), channel_id=1, source_target_pairs={{1,0},{2,1},{3,2},{4,3},{5,4},{6,5},{7,6},{8,7},{9,8},{10,9},{11,1... | collective-permute-start | bytes 1568 | tf_op jit(solution)/shard_map/ppermute | solution.py:39
  220.5 17.5 %all-to-all-start.4 = ((f32[64,1,128]{2,1,0:T(1,128)}), f32[64,1,128]{2,1,0:T(1,128)S(1)}, u32[]{:S(2)}, u32[]{:S(2)}) async-start(f32[64,1,128]{2,1,0:T(1,128)} %broadcast_in_dim.96), calls=%async_computation.4 | async-start | bytes 65536 | tf_op jit(solution)/shard_map/all_to_all | solution.py:52
  289.5 12.5 %collective-permute-start.11 = (f32[130,1]{0,1:T(1,128)S(1)}, f32[130,1]{0,1:T(1,128)S(1)}, u32[]{:S(2)}, u32[]{:S(2)}) collective-permute-start(f32[130,1]{0,1:T(1,128)S(1)} %get-tuple-element.507), channel_id=1, source_target_pairs={{0,1},{1,2},{2,3},{3,4},{4,5},{5,6},{6,7},{7,8},{8,9},{9,10},{10,1... | collective-permute-start | bytes 1568 | tf_op jit(solution)/shard_map/ppermute | solution.py:38
  294.0 17.5 %all-to-all-start.5 = ((f32[64,1,128]{2,1,0:T(1,128)}), f32[64,1,128]{2,1,0:T(1,128)S(1)}, u32[]{:S(2)}, u32[]{:S(2)}) async-start(f32[64,1,128]{2,1,0:T(1,128)} %broadcast_in_dim.97), calls=%async_computation.5 | async-start | bytes 65536 | tf_op jit(solution)/shard_map/all_to_all | solution.py:52
  363.0 12.3 %collective-permute-start.13 = (f32[130,1]{0,1:T(1,128)S(1)}, f32[130,1]{0,1:T(1,128)S(1)}, u32[]{:S(2)}, u32[]{:S(2)}) collective-permute-start(f32[130,1]{0,1:T(1,128)S(1)} %get-tuple-element.503), channel_id=1, source_target_pairs={{0,1},{1,2},{2,3},{3,4},{4,5},{5,6},{6,7},{7,8},{8,9},{9,10},{10,1... | collective-permute-start | bytes 1568 | tf_op jit(solution)/shard_map/ppermute | solution.py:38
  367.2 17.5 %all-to-all-start.6 = ((f32[64,1,128]{2,1,0:T(1,128)}), f32[64,1,128]{2,1,0:T(1,128)S(1)}, u32[]{:S(2)}, u32[]{:S(2)}) async-start(f32[64,1,128]{2,1,0:T(1,128)} %broadcast_in_dim.98), calls=%async_computation.6 | async-start | bytes 65536 | tf_op jit(solution)/shard_map/all_to_all | solution.py:52
  436.1 12.3 %collective-permute-start.15 = (f32[130,1]{0,1:T(1,128)S(1)}, f32[130,1]{0,1:T(1,128)S(1)}, u32[]{:S(2)}, u32[]{:S(2)}) collective-permute-start(f32[130,1]{0,1:T(1,128)S(1)} %get-tuple-element.499), channel_id=1, source_target_pairs={{0,1},{1,2},{2,3},{3,4},{4,5},{5,6},{6,7},{7,8},{8,9},{9,10},{10,1... | collective-permute-start | bytes 1568 | tf_op jit(solution)/shard_map/ppermute | solution.py:38
  439.5 8.9 %collective-permute-start.14 = (f32[130,1]{0,1:T(1,128)S(1)}, f32[130,1]{0,1:T(1,128)S(1)}, u32[]{:S(2)}, u32[]{:S(2)}) collective-permute-start(f32[130,1]{0,1:T(1,128)S(1)} %get-tuple-element.500), channel_id=1, source_target_pairs={{1,0},{2,1},{3,2},{4,3},{5,4},{6,5},{7,6},{8,7},{9,8},{10,9},{11,1... | collective-permute-start | bytes 1568 | tf_op jit(solution)/shard_map/ppermute | solution.py:39
  440.3 17.5 %all-to-all-start.7 = ((f32[64,1,128]{2,1,0:T(1,128)}), f32[64,1,128]{2,1,0:T(1,128)S(1)}, u32[]{:S(2)}, u32[]{:S(2)}) async-start(f32[64,1,128]{2,1,0:T(1,128)} %broadcast_in_dim.99), calls=%async_computation.7 | async-start | bytes 65536 | tf_op jit(solution)/shard_map/all_to_all | solution.py:52
  509.6 12.3 %collective-permute-start.17 = (f32[130,1]{0,1:T(1,128)S(1)}, f32[130,1]{0,1:T(1,128)S(1)}, u32[]{:S(2)}, u32[]{:S(2)}) collective-permute-start(f32[130,1]{0,1:T(1,128)S(1)} %get-tuple-element.495), channel_id=1, source_target_pairs={{0,1},{1,2},{2,3},{3,4},{4,5},{5,6},{6,7},{7,8},{8,9},{9,10},{10,1... | collective-permute-start | bytes 1568 | tf_op jit(solution)/shard_map/ppermute | solution.py:38
  513.8 17.5 %all-to-all-start.8 = ((f32[64,1,128]{2,1,0:T(1,128)}), f32[64,1,128]{2,1,0:T(1,128)S(1)}, u32[]{:S(2)}, u32[]{:S(2)}) async-start(f32[64,1,128]{2,1,0:T(1,128)} %broadcast_in_dim.100), calls=%async_computation.8 | async-start | bytes 65536 | tf_op jit(solution)/shard_map/all_to_all | solution.py:52
  582.8 12.3 %collective-permute-start.19 = (f32[130,1]{0,1:T(1,128)S(1)}, f32[130,1]{0,1:T(1,128)S(1)}, u32[]{:S(2)}, u32[]{:S(2)}) collective-permute-start(f32[130,1]{0,1:T(1,128)S(1)} %get-tuple-element.491), channel_id=1, source_target_pairs={{0,1},{1,2},{2,3},{3,4},{4,5},{5,6},{6,7},{7,8},{8,9},{9,10},{10,1... | collective-permute-start | bytes 1568 | tf_op jit(solution)/shard_map/ppermute | solution.py:38
  587.0 17.5 %all-to-all-start.9 = ((f32[64,1,128]{2,1,0:T(1,128)}), f32[64,1,128]{2,1,0:T(1,128)S(1)}, u32[]{:S(2)}, u32[]{:S(2)}) async-start(f32[64,1,128]{2,1,0:T(1,128)} %broadcast_in_dim.101), calls=%async_computation.9 | async-start | bytes 65536 | tf_op jit(solution)/shard_map/all_to_all | solution.py:52
  (7 other events, 95.2 us)
where the time goes:
time: 659 us; the launch traced here: 649 us
  blocking collectives  350 us (53%)
  starting transfers between devices  110 us (17%)
  waiting for transfers between devices  86.9 us (13%)
  local copies, waits for them, and re-layouts  46.4 us (7%)
  between operations  32.6 us (5%)
  other arithmetic  23.6 us (4%)
    psum x32, blocking collectives, one_axis_at_a_time(): return functools.reduce(lax.psum, axes, shard)  293 us
    all_to_all x10, waiting for transfers between devices, copy_for_each(): return lax.all_to_all(copies, axis, split_axis=0, concat_axis=0, tiled=True)  80 us
    all_to_all x10, starting transfers between devices, copy_for_each(): return lax.all_to_all(copies, axis, split_axis=0, concat_axis=0, tiled=True)  77.1 us
    all_gather x8, blocking collectives, precondition(): gathered_ends = lax.all_gather(end_values, 'lat', axis=0, tiled=True)  56.5 us
    ppermute x10, starting transfers between devices, with_halo(): before = lax.ppermute(last, axis, up)  27 us
  transfers between devices with their start and end apart: 30, of which 12 were waited for; matrix products, arithmetic and copies ran while one was open for 3% of the time, Pallas kernels for 0%

commit v1 on v0

v1 whole, which is shorter than its diff:
```python
import functools

import jax
import jax.numpy as jnp
from jax import lax
from jax.experimental import pallas as pl
from jax.experimental.pallas import tpu as pltpu
from jax.sharding import Mesh
from jax.sharding import PartitionSpec as P

LON = ("x", "z", "core")
NLON = 8192
COLS = 128
OWN = 32
GHOST = 8
WIDE = OWN + 2 * GHOST
PAD = COLS + 2 * GHOST
STEPS = 64
HALF = 4
TOTAL = 2 * HALF
SCALE = 1.0e-4
F32 = jnp.float32
HIGHEST = lax.Precision.HIGHEST
E, W, N, S, NE, SW, NW, SE, DIAG = range(9)
MULT, IPIV, LOWER, UPPER = range(4)


def params():
    return pltpu.CompilerParams(vmem_limit_bytes=48 * 1024 * 1024)


def two_sum(a, b):
    s = a + b
    bb = s - a
    return s, (a - (s - bb)) + (b - bb)


def split(a):
    t = a * 4097.0
    hi = t - (t - a)
    return hi, a - hi


def two_prod(a, b):
    p = a * b
    ah, al = split(a)
    bh, bl = split(b)
    return p, ((ah * bh - p) + ah * bl + al * bh) + al * bl


def renorm(s, e):
    hi = s + e
    return hi, e - (hi - s)


def pair_sub(a, b):
    s, e = two_sum(a[0], -b[0])
    return renorm(s, e + (a[1] - b[1]))


def pair_mul(a, b):
    p, e = two_prod(a[0], b[0])
    return renorm(p, e + (a[0] * b[1] + a[1] * b[0]))


def pair_div(a, b):
    first = a[0] / b[0]
    zero = jnp.zeros_like(first)
    rest = pair_sub(a, pair_mul((first, zero), b))
    return renorm(first, rest[0] / b[0])


def sum_rows(values):
    s = values[0:8]
    e = jnp.zeros_like(s)
    for start in range(8, values.shape[0], 8):
        s, err = two_sum(s, values[start : start + 8])
        e = e + err
    for shift in (4, 2, 1):
        s_other = pltpu.roll(s, shift, 0)
        e_other = pltpu.roll(e, shift, 0)
        s, err = two_sum(s, s_other)
        e = e + e_other + err
    hi, lo = renorm(s, e)
    return hi[0:1], lo[0:1]


def small_solve(hi_row, lo_row, order):
    row = lax.broadcasted_iota(jnp.int32, (8, 128), 0)
    lane = lax.broadcasted_iota(jnp.int32, (8, 128), 1)

    def matrix(values):
        wide = jnp.broadcast_to(values, (8, 128))
        out = jnp.zeros((8, 128), F32)
        for i in range(order):
            turned = wide if i == 0 else pltpu.roll(wide, 128 - 16 * i, 1)
            out = jnp.where(row == i, turned, out)
        return jnp.where(lane < 16, out, 0.0)

    hi, lo = matrix(hi_row), matrix(lo_row)
    ratio = hi[3:4, 3:4] / hi[3:4, 2:3]
    start = jnp.sum(jnp.where(row == lane, hi, 0.0), axis=1, keepdims=True)
    unit = jnp.where(row == lane, 1.0, 0.0)
    live = jnp.ones((8, 128), F32)
    for k in range(order):
        col = tuple(jnp.broadcast_to(v[:, k : k + 1], (8, 128)) for v in (hi, lo))
        piv_row = tuple(jnp.broadcast_to(v[k : k + 1, :], (8, 128)) for v in (hi, lo))
        piv = tuple(jnp.broadcast_to(v[k : k + 1, k : k + 1], (8, 128)) for v in (hi, lo))
        good = piv[0] > 1e-11 * jnp.broadcast_to(start[k : k + 1, :], (8, 128))
        piv = (jnp.where(good, piv[0], 1.0), jnp.where(good, piv[1], 0.0))
        factor = pair_div(col, piv)
        new = pair_sub((hi, lo), pair_mul(factor, piv_row))
        change = good & (row != k)
        hi = jnp.where(change, new[0], hi)
        lo = jnp.where(change, new[1], lo)
        live = jnp.where((row == k) & ~good, 0.0, live)
    diag = jnp.sum(jnp.where(row == lane, hi, 0.0), axis=1, keepdims=True)
    diag = jnp.where((diag != 0.0) & (live[:, 0:1] > 0.0), diag, 1.0)
    y = jnp.broadcast_to(hi[:, 8:9] / diag, (8, 128)) * live
    y = jnp.where(row < order, y, 0.0)
    del unit
    return y, jnp.broadcast_to(ratio, (8, 128))


def pack_body(rhs, surface, east, north, neast, nwest, land, out):
    for place, ref in enumerate((rhs, surface, east, north, neast, nwest)):
        out[place] = ref[...].T
    out[6] = land[...].astype(F32).T


def select_body(offset, ghosted, first, second, out):
    rho = offset[0, 0]
    same = offset[0, 1]
    i = lax.broadcasted_iota(jnp.int32, (PAD, 2 * 136), 0)
    u = lax.broadcasted_iota(jnp.int32, (PAD, 2 * 136), 1)
    plain = jnp.where(u == rho + PAD - i, 1.0, 0.0)
    moved = jnp.where(u == rho + PAD - 1 - i, 1.0, 0.0)
    for place, source in enumerate((0, 1, 2, 3, 5, 4, 6)):
        x, y = first[source], second[source]
        low = jnp.where(same == 0, y, x)
        high = jnp.where(same == 0, x, y)
        both = jnp.concatenate([low[0:136], high[8:PAD]], axis=0)
        facing = jnp.dot(moved if source == 2 else plain, both, precision=HIGHEST, preferred_element_type=F32)
        for part in range(4):
            out[part, place, 0:WIDE, :] = ghosted[place, OWN * part : OWN * part + WIDE, :]
            out[part, place, WIDE : 2 * WIDE, :] = facing[OWN * part : OWN * part + WIDE, :]


def east_of(v):
    return pltpu.roll(v, 127, v.ndim - 1)


def west_of(v):
    return pltpu.roll(v, 1, v.ndim - 1)


def facing_of(v):
    return pltpu.roll(v, 64, v.ndim - 1)


def row_before(v):
    s = lax.broadcasted_iota(jnp.int32, (8, 128), 0)
    return jnp.where(s == 0, 0.0, pltpu.roll(v, 1, 0))


def row_after(v):
    s = lax.broadcasted_iota(jnp.int32, (8, 128), 0)
    return jnp.where(s == 7, 0.0, pltpu.roll(v, 7, 0))


def line_solve(load, lines, below_mat, above_mat, y_buf, g_buf, finish):
    zero = jnp.zeros((8, 128), F32)

    def forward(t, y):
        y = load(t) + lines[MULT, t] * y
        y_buf[t] = y
        return y

    lax.fori_loop(0, STEPS, forward, zero, unroll=8)

    def backward(k, x):
        t = STEPS - 1 - k
        x = y_buf[t] * lines[IPIV, t] + lines[MULT, t + 1] * x
        g_buf[t] = x
        return x

    lax.fori_loop(0, STEPS, backward, zero, unroll=8)
    first, last = g_buf[0], g_buf[STEPS - 1]
    below, above = zero, zero
    for k in range(8):
        for base, ends in ((0, first), (8, last)):
            end = jnp.broadcast_to(ends[k : k + 1, :], (8, 128))
            below = below + below_mat[base + k] * end
            above = above + above_mat[base + k] * end

    def combine(c, _):
        t0 = c * 8
        g = g_buf[pl.ds(t0, 8)] + lines[LOWER, pl.ds(t0, 8)] * below + lines[UPPER, pl.ds(t0, 8)] * above
        finish(t0, g)
        return 0

    lax.fori_loop(0, STEPS // 8, combine, 0, unroll=2)


def operate(v_ref, place, w_ref, coef, fold, vp, ve, vw):
    for t, v in ((0, row_before(v_ref[place, STEPS - 1])), (STEPS + 1, row_after(v_ref[place, 0]))):
        vp[t] = v
        ve[t] = east_of(v)
        vw[t] = west_of(v)

    def step(c, _):
        t = c * 4
        here, up, down = pl.ds(t + 1, 4), pl.ds(t + 2, 4), pl.ds(t, 4)
        at = pl.ds(t, 4)
        out = coef[DIAG, at] * vp[here]
        side = coef[E, at] * ve[here] + coef[W, at] * vw[here]
        north = coef[N, at] * vp[up] + coef[NE, at] * ve[up] + coef[NW, at] * vw[up]
        south = coef[S, at] * vp[down] + coef[SW, at] * vw[down] + coef[SE, at] * ve[down]
        w_ref[place, at] = out - (side + north + south)
        return 0

    lax.fori_loop(0, STEPS // 4, step, 0, unroll=2)
    w_ref[place, STEPS - 1] = w_ref[place, STEPS - 1] - fold[...] * facing_of(v_ref[place, STEPS - 1])


def store_field(v_ref, place, vp, ve, vw):
    def finish_with(value_of):
        def finish(t0, g):
            v = value_of(t0, g)
            v_ref[place, pl.ds(t0, 8)] = v
            vp[pl.ds(t0 + 1, 8)] = v
            ve[pl.ds(t0 + 1, 8)] = east_of(v)
            vw[pl.ds(t0 + 1, 8)] = west_of(v)

        return finish

    return finish_with


def gram_row(entries, rows, out):
    lane = lax.broadcasted_iota(jnp.int32, (8, 128), 1)
    own = (lane >= GHOST) & (lane < GHOST + OWN)
    rows[...] = jnp.zeros((128, 128), F32)
    group = 16
    for start in range(0, len(entries), group):
        part = entries[start : start + group]

        def add(t, sums, part=part):
            return tuple(s + left(t) * right(t) for s, (left, right, _) in zip(sums, part))

        sums = lax.fori_loop(0, STEPS, add, tuple(jnp.zeros((8, 128), F32) for _ in part), unroll=2)
        for total, (_, _, places) in zip(sums, part):
            line = jnp.sum(jnp.where(own, total, 0.0), axis=0, keepdims=True)
            for place in places:
                rows[place : place + 1, :] = line
    summed = lax.dot_general(
        jnp.ones((8, 128), F32), rows[...], (((1,), (1,)), ((), ())), precision=HIGHEST, preferred_element_type=F32
    )
    out[...] = jnp.concatenate([summed] * 4, axis=0)


def at(ref, *index):
    return lambda t: ref[(*index, t)]


def first_body(recv, coef, lines, below_mat, above_mat, fold, r0, v_ref, w_ref, gram, raw, grid, y_buf, g_buf, vp, ve, vw, rows):
    s_id = lax.broadcasted_iota(jnp.int32, (8, 128), 0)
    zero = jnp.zeros((8, 128), F32)
    gap = jnp.zeros((64 - WIDE, 128), F32)
    for place in range(7):
        for source in range(4):
            both = recv[source, place]
            full = jnp.concatenate([both[0:WIDE], gap, both[WIDE : 2 * WIDE], gap], axis=0)
            raw[place, 128 * source : 128 * source + 128, :] = full.T
        for t in range(STEPS):
            grid[place, t + 1] = raw[place, pl.ds(t, 8, stride=STEPS), :]
    top_north = grid[3, STEPS]
    top_ocean = grid[6, STEPS]
    last = s_id == 7
    fold_open = jnp.where(last, 0.5 * (top_north + facing_of(top_north)), 0.0)
    fold[...] = fold_open * top_ocean * facing_of(top_ocean)
    for place in (3, 4, 5):
        grid[place, STEPS] = jnp.where(last, 0.0, grid[place, STEPS])
    for place in (3, 4, 5, 6):
        grid[place, 0] = row_before(grid[place, STEPS])
        grid[place, STEPS + 1] = row_after(grid[place, 1])

    def weigh(t, _):
        o, o_up, o_down = grid[6, t + 1], grid[6, t + 2], grid[6, t]
        east = grid[2, t + 1]
        north, neast, nwest = grid[3, t + 1], grid[4, t + 1], grid[5, t + 1]
        south, s_neast, s_nwest = grid[3, t], grid[4, t], grid[5, t]
        open_sum = zero
        parts = (
            (E, east, east_of(o)),
            (W, west_of(east), west_of(o)),
            (N, north, o_up),
            (S, south, o_down),
            (NE, neast, east_of(o_up)),
            (SW, west_of(s_neast), west_of(o_down)),
            (NW, nwest, west_of(o_up)),
            (SE, east_of(s_nwest), east_of(o_down)),
        )
        for place, edge, other in parts:
            coef[place, t] = edge * o * other
            open_sum = open_sum + edge
        surface = grid[1, t + 1]
        coef[DIAG, t] = o * (surface + open_sum) + (1.0 - o)
        r0[t] = o * grid[0, t + 1]
        y_buf[t] = o * (surface + north * o * o_up + south * o * o_down) + (1.0 - o)
        return 0

    lax.fori_loop(0, STEPS, weigh, 0, unroll=2)
    surface = grid[1, STEPS]
    o = top_ocean
    coef[DIAG, STEPS - 1] = coef[DIAG, STEPS - 1] + o * fold_open

    def pivots(t, carry):
        before, response = carry
        south = jnp.where(t == 0, zero, coef[S, t])
        mult = south * before
        inverse = 1.0 / (y_buf[t] - south * mult)
        lines[MULT, t] = mult
        lines[IPIV, t] = inverse
        response = jnp.where(t == 0, coef[S, 0], mult * response)
        g_buf[t] = response
        return inverse, response

    lax.fori_loop(0, STEPS, pivots, (zero, zero), unroll=4)
    for t in range(STEPS, lines.shape[1]):
        lines[MULT, t] = zero

    def respond(k, carry):
        low, up = carry
        t = STEPS - 1 - k
        factor = lines[MULT, t + 1]
        low = g_buf[t] * lines[IPIV, t] + factor * low
        up = jnp.where(k == 0, coef[N, STEPS - 1] * lines[IPIV, t], factor * up)
        lines[LOWER, t] = low
        lines[UPPER, t] = up
        return low, up

    lax.fori_loop(0, STEPS, respond, (zero, zero), unroll=4)
    unit = lax.broadcasted_iota(jnp.int32, (16, 128), 0)
    low_first, low_last = lines[LOWER, 0], lines[LOWER, STEPS - 1]
    up_first, up_last = lines[UPPER, 0], lines[UPPER, STEPS - 1]

    def spread(v, s):
        return jnp.broadcast_to(v[s : s + 1, :], (16, 128))

    alphas, betas, dens = [jnp.zeros((16, 128), F32)], [jnp.zeros((16, 128), F32)], []
    for s in range(8):
        alpha, beta = alphas[-1], betas[-1]
        g_first = jnp.where(unit == s, 1.0, 0.0)
        g_last = jnp.where(unit == 8 + s, 1.0, 0.0)
        lf, ll, uf, ul = (spread(v, s) for v in (low_first, low_last, up_first, up_last))
        den = 1.0 / (1.0 - lf * beta)
        dens.append(den)
        alphas.append(g_last + ll * (alpha + beta * den * (g_first + lf * alpha)))
        betas.append(ul + ll * beta * den * uf)
    above = jnp.zeros((16, 128), F32)
    for s in range(7, -1, -1):
        alpha, beta = alphas[s], betas[s]
        above_mat[:, s, :] = above
        lf, uf = spread(low_first, s), spread(up_first, s)
        g_first = jnp.where(unit == s, 1.0, 0.0)
        above = dens[s] * (g_first + lf * alpha + uf * above)
        below_mat[:, s, :] = alpha + beta * above
    finish_with = functools.partial(store_field, v_ref)
    for i in range(HALF):
        load = (lambda t: r0[t]) if i == 0 else (lambda t, i=i: w_ref[i - 1, t])
        value = (lambda t0, g: g) if i == 0 else (lambda t0, g: g * SCALE)
        line_solve(load, lines, below_mat, above_mat, y_buf, g_buf, finish_with(i, vp, ve, vw)(value))
        operate(v_ref, i, w_ref, coef, fold, vp, ve, vw)
    entries = []
    for i in range(HALF):
        for j in range(i, HALF):
            entries.append((at(v_ref, i), at(w_ref, j), sorted({16 * i + j, 16 * j + i})))
        entries.append((at(v_ref, i), lambda t: r0[t], [16 * i + 8]))
    gram_row(entries, rows, gram)


def second_body(sums, coef, lines, below_mat, above_mat, fold, r0, v1, w1, r_ref, y_out, v_ref, w_ref, gram, y_buf, g_buf, vp, ve, vw, rows):
    y, ratio = small_solve(*sum_rows(sums[...]), HALF)
    y_out[...] = y
    bound = ratio * (1.6 / SCALE)
    step = 2.0 / bound
    weights = [jnp.broadcast_to(y[i : i + 1, :], (8, 128)) for i in range(HALF)]

    def renew(t, _):
        r = r0[t]
        for i in range(HALF):
            r = r - weights[i] * w1[i, t]
        r_ref[t] = r
        return 0

    lax.fori_loop(0, STEPS, renew, 0, unroll=4)
    finish_with = functools.partial(store_field, v_ref)
    for i in range(HALF):
        load = (lambda t: r_ref[t]) if i == 0 else (lambda t, i=i: w_ref[i - 1, t])
        if i == 0:
            value = lambda t0, g: g
        elif i == 1:
            value = lambda t0, g: v_ref[0, pl.ds(t0, 8)] - step * g
        else:
            value = lambda t0, g, i=i: 2.0 * (v_ref[i - 1, pl.ds(t0, 8)] - step * g) - v_ref[i - 2, pl.ds(t0, 8)]
        line_solve(load, lines, below_mat, above_mat, y_buf, g_buf, finish_with(i, vp, ve, vw)(value))
        operate(v_ref, i, w_ref, coef, fold, vp, ve, vw)
    entries = []
    for i in range(TOTAL):
        left = at(v1, i) if i < HALF else at(v_ref, i - HALF)
        for j in range(i, TOTAL):
            right = at(w1, j) if j < HALF else at(w_ref, j - HALF)
            entries.append((left, right, sorted({16 * i + j, 16 * j + i})))
        entries.append((left, lambda t: r_ref[t], [16 * i + 8]))
    gram_row(entries, rows, gram)


def middle_body(values, out):
    hi, lo = sum_rows(values[...])
    row = lax.broadcasted_iota(jnp.int32, (16, 128), 0)
    even = (row & 1) == 0
    out[...] = jnp.where(even, jnp.broadcast_to(hi, (16, 128)), jnp.broadcast_to(lo, (16, 128)))


def last_body(sums, y1, r_ref, v1, w1, v2, w2, out, x_rows, r_rows):
    y, _ = small_solve(*sum_rows(sums[...]), TOTAL)
    w_weights = [jnp.broadcast_to(y[i : i + 1, :], (8, 128)) for i in range(TOTAL)]
    v_weights = [w + (y1[i : i + 1, :] if i < HALF else 0.0) for i, w in enumerate(w_weights)]
    for t in range(STEPS):
        x = jnp.zeros((8, 128), F32)
        r = r_ref[t]
        for i in range(HALF):
            x = x + v_weights[i] * v1[i, t]
            r = r - w_weights[i] * w1[i, t]
        for i in range(HALF):
            x = x + v_weights[HALF + i] * v2[i, t]
            r = r - w_weights[HALF + i] * w2[i, t]
        x_rows[pl.ds(t, 8, stride=STEPS), :] = x
        r_rows[pl.ds(t, 8, stride=STEPS), :] = r
    for place, rows in enumerate((x_rows, r_rows)):
        for part in range(4):
            out[part, place] = rows[128 * part : 128 * part + 128, :].T[GHOST : GHOST + OWN, :]


def unpack_body(recv, x, r):
    for place, ref in enumerate((x, r)):
        ref[...] = jnp.concatenate([recv[part, place] for part in range(4)], axis=0).T


def shape(*dims):
    return jax.ShapeDtypeStruct(dims, F32)


def vmem(*dims):
    return pltpu.VMEM(dims, F32)


FIELD = (STEPS, 8, 128)
SCRATCH = [vmem(*FIELD), vmem(*FIELD), vmem(STEPS + 2, 8, 128), vmem(STEPS + 2, 8, 128), vmem(STEPS + 2, 8, 128), vmem(128, 128)]


def all_sums(gram):
    near = lax.all_to_all(gram, ("lat", "x", "core"), split_axis=0, concat_axis=0, tiled=True)
    part = pl.pallas_call(middle_body, out_shape=shape(16, 128), name="add_near")(near)
    return lax.all_to_all(part, "z", split_axis=0, concat_axis=0, tiled=True)


def reflect_switch(block, half):
    def branch(q):
        return lambda b: lax.ppermute(b, LON, [(d, (2 * q - d) % 64) for d in range(64)])

    return lax.switch(half, [branch(q) for q in range(32)], block)


def shards(right_side, surface_term, east, north, neast, nwest, land_sea, fold_map):
    place = lax.axis_index(LON)
    offset = (fold_map[0] + COLS * place) % NLON
    block_offset = offset // COLS
    rho = offset % COLS
    odd = block_offset % 2
    packed = pl.pallas_call(pack_body, out_shape=shape(7, COLS, 128), name="pack")(
        right_side, surface_term, east, north, neast, nwest, land_sea
    )
    up = [(d, (d + 1) % 64) for d in range(64)]
    down = [(d, (d - 1) % 64) for d in range(64)]
    before = lax.ppermute(packed[:, COLS - GHOST :], LON, up)
    after = lax.ppermute(packed[:, :GHOST], LON, down)
    ghosted = jnp.concatenate([before, packed, after], axis=1)
    first = reflect_switch(ghosted, block_offset // 2)
    second = lax.cond(
        odd == 0, lambda b: lax.ppermute(b, LON, down), lambda b: lax.ppermute(b, LON, up), first
    )
    scalars = jnp.stack([rho, odd]).reshape(1, 2)
    windows = pl.pallas_call(
        select_body,
        in_specs=[pl.BlockSpec(memory_space=pltpu.SMEM)] + [pl.BlockSpec(memory_space=pltpu.VMEM)] * 3,
        out_shape=shape(4, 7, 2 * WIDE, 128),
        name="select",
        compiler_params=params(),
    )(scalars, ghosted, first, second)
    lines_in = lax.all_to_all(windows, "lat", split_axis=0, concat_axis=0, tiled=True)
    coef, lines, below_mat, above_mat, fold, r0, v1, w1, gram = pl.pallas_call(
        first_body,
        out_shape=(
            shape(9, *FIELD),
            shape(4, STEPS + 8, 8, 128),
            shape(16, 8, 128),
            shape(16, 8, 128),
            shape(8, 128),
            shape(*FIELD),
            shape(HALF, *FIELD),
            shape(HALF, *FIELD),
            shape(32, 128),
        ),
        scratch_shapes=[vmem(7, 512, 128), vmem(7, STEPS + 2, 8, 128), *SCRATCH],
        name="phase_one",
        compiler_params=params(),
    )(lines_in)
    sums = all_sums(gram)
    r4, y1, v2, w2, gram = pl.pallas_call(
        second_body,
        out_shape=(
            shape(*FIELD),
            shape(8, 128),
            shape(HALF, *FIELD),
            shape(HALF, *FIELD),
            shape(32, 128),
        ),
        scratch_shapes=SCRATCH,
        name="phase_two",
        compiler_params=params(),
    )(sums, coef, lines, below_mat, above_mat, fold, r0, v1, w1)
    sums = all_sums(gram)
    pieces = pl.pallas_call(
        last_body,
        out_shape=shape(4, 2, OWN, 128),
        scratch_shapes=[vmem(512, 128), vmem(512, 128)],
        name="combine",
        compiler_params=params(),
    )(sums, y1, r4, v1, w1, v2, w2)
    columns = lax.all_to_all(pieces, "lat", split_axis=0, concat_axis=0, tiled=True)
    return pl.pallas_call(unpack_body, out_shape=(shape(128, COLS), shape(128, COLS)), name="unpack")(columns)


def solution(mesh):
    finer = Mesh(mesh.devices.reshape(mesh.shape["lat"], 4, 8, 2), ("lat", *LON))
    field = P("lat", LON)
    return jax.shard_map(
        shards,
        mesh=finer,
        in_specs=(field,) * 7 + (P(LON),),
        out_specs=(field, field),
        check_vma=False,
    )
```

time: 659 us -> 164 us (0.25); the launches traced: 649 us -> 163 us
  blocking collectives: 350 us -> 75.8 us
  starting transfers between devices: 110 us -> 9.28 us
  waiting for transfers between devices: 86.9 us -> 34.2 us
  local copies, waits for them, and re-layouts: 46.4 us -> 9.84 us
  Pallas kernels: 0 us -> 31.6 us
  between operations: 32.6 us -> 1.38 us
  other arithmetic: 23.6 us -> 1.13 us
    psum x32 -> x0, blocking collectives: 293 us -> none  [one_axis_at_a_time(): return functools.reduce(lax.psum, axes, shard)]
    all_to_all x10 -> x0, waiting for transfers between devices: 80 us -> none  [copy_for_each(): return lax.all_to_all(copies, axis, split_axis=0, concat_axis=0, tiled=True)]
    all_to_all x10 -> x0, starting transfers between devices: 77.1 us -> none  [copy_for_each(): return lax.all_to_all(copies, axis, split_axis=0, concat_axis=0, tiled=True)]
    all_to_all x0 -> x6, blocking collectives: none -> 75.8 us  [the longest x2 25.5 us: all_sums(): lax.all_to_all(gram, ('lat', 'x', 'core'), split_axis=0, concat_axis=0, t...]
    all_gather x8 -> x0, blocking collectives: 56.5 us -> none  [precondition(): gathered_ends = lax.all_gather(end_values, 'lat', axis=0, tiled=True)]
    pallas_call x0 -> x8, Pallas kernels: none -> 31.6 us  [the longest x1 11.7 us: shards(): pl.pallas_call(first_body, out_shape=(shape(9, *FIELD), shape(4, STEPS +...]
    ppermute x20 -> x4, waiting for transfers between devices: 6.9 us -> 34.2 us  [the longest x1 23.2 us: branch(): lax.ppermute(b, LON, [(d, (2 * q - d) % 64) for d in range(64)])]
    ppermute x20 -> x4, starting transfers between devices: 32.5 us -> 9.28 us  [the longest x1 6.01 us: branch(): lax.ppermute(b, LON, [(d, (2 * q - d) % 64) for d in range(64)])]
  transfers between devices with their start and end apart: 30 -> 4, of which waited for: 12 -> 3; matrix products, arithmetic and copies ran while one was open for 3% -> 0% of each run, Pallas kernels for 0% -> 0%
where the time goes in v1:
time: 164 us; the launch traced here: 163 us
  blocking collectives  75.8 us (46%)
  waiting for transfers between devices  34.2 us (21%)
  Pallas kernels  31.6 us (19%)
  local copies, waits for them, and re-layouts  9.84 us (6%)
  starting transfers between devices  9.28 us (6%)
    all_to_all x2, blocking collectives, all_sums(): lax.all_to_all(gram, ('lat', 'x', 'core'), split_axis=0, concat_axis=0, t...  25.5 us
    ppermute x1, waiting for transfers between devices, branch(): lax.ppermute(b, LON, [(d, (2 * q - d) % 64) for d in range(64)])  23.2 us
    all_to_all x1, blocking collectives, shards(): lax.all_to_all(windows, 'lat', split_axis=0, concat_axis=0, tiled=True)  21.3 us
    all_to_all x2, blocking collectives, all_sums(): return lax.all_to_all(part, 'z', split_axis=0, concat_axis=0, tiled=True)  21.1 us
    pallas_call x1, Pallas kernels, shards(): pl.pallas_call(first_body, out_shape=(shape(9, *FIELD), shape(4, STEPS +...  11.7 us
    unnamed x20, local copies, waits for them, and re-layouts  9.07 us
    pallas_call x1, Pallas kernels, shards(): pl.pallas_call(second_body, out_shape=(shape(*FIELD), shape(8, 128), shap...  8.89 us
    ppermute x1, waiting for transfers between devices, shards(): lax.ppermute(b, LON, down)  8.83 us
  transfers between devices with their start and end apart: 4, of which 3 were waited for; matrix products, arithmetic and copies ran while one was open for 0% of the time, Pallas kernels for 0%

profile of v1, /device:TPU:1, one launch (start us, length us, event | category | flops | bytes accessed | tf_op | source)
XLA Modules:
  0.0 163.3 jit_solution(8564689691127457430)
XLA Ops:
  0.6 2.0 %pack.1 = f32[7,128,128]{2,1,0:T(8,128)} custom-call(f32[128,128]{1,0:T(8,128)} %rhs.1, f32[128,128]{1,0:T(8,128)} %surface.1, f32[128,128]{1,0:T(8,128)} %east.1, f32[128,128]{1,0:T(8,128)} %north.1, f32[128,128]{1,0:T(8,128)} %neast.1, f32[128,128]{1,0:T(8,128)} %nwest.1, s32[128,128]{1,0:T(8,128)} %land.1), custom_call_target="tpu_custom_call" | custom-call | tf_op jit(solution)/shard_map/pack/pallas_call | solution.py:482
  3.4 3.0 %collective-permute-start.34 = (f32[7,8,128]{2,1,0:T(8,128)S(1)}, f32[7,8,128]{2,1,0:T(8,128)S(1)}, u32[]{:S(2)}, u32[]{:S(2)}) collective-permute-start(f32[7,8,128]{2,1,0:T(8,128)S(1)} %get-tuple-element.100), channel_id=1, source_target_pairs={{0,1},{1,2},{2,3},{3,4},{4,5},{5,6},{6,7},{7,8},{8,9},{9,10},{10,1... | collective-permute-start | bytes 86024 | tf_op jit(solution)/shard_map/ppermute | solution.py:487
  7.5 2.2 %collective-permute-done.35 = f32[7,8,128]{2,1,0:T(8,128)S(1)} collective-permute-done((f32[7,8,128]{2,1,0:T(8,128)S(1)}, f32[7,8,128]{2,1,0:T(8,128)S(1)}, u32[]{:S(2)}, u32[]{:S(2)}) %collective-permute-start.35) | collective-permute-done | bytes 28704 | tf_op jit(solution)/shard_map/ppermute | solution.py:488
  9.7 1.1 pad_maximum_fusion.ghosted
  10.8 29.2 %conditional.2 = (f32[7,144,128]{2,1,0:T(8,128)}) conditional(s32[]{:T(128)} %clamp.3, f32[7,144,128]{2,1,0:T(8,128)S(1)} %pad_maximum_fusion.ghosted, f32[7,144,128]{2,1,0:T(8,128)S(1)} %pad_maximum_fusion.ghosted, f32[7,144,128]{2,1,0:T(8,128)S(1)} %pad_maximum_fusion.ghosted, ...), branch_computations={%region_0.1_spmd, %region_1.2_spmd, %region_2.3_spmd, %region_3.4_... | conditional | bytes 2064432 | solution.py:473
  10.8 6.0 %collective-permute-start.18 = (f32[7,144,128]{2,1,0:T(8,128)S(1)}, f32[7,144,128]{2,1,0:T(8,128)}, u32[]{:S(2)}, u32[]{:S(2)}) collective-permute-start(f32[7,144,128]{2,1,0:T(8,128)S(1)} %param.18), channel_id=1, source_target_pairs={{0,36},{1,35},{2,34},{3,33},{4,32},{5,31},{6,30},{7,29},{8,28},{9,... | collective-permute-start | bytes 1548296 | tf_op jit(solution)/shard_map/cond/branch_18_fun/ppermute | solution.py:471
  16.8 23.2 %collective-permute-done.18 = f32[7,144,128]{2,1,0:T(8,128)} collective-permute-done((f32[7,144,128]{2,1,0:T(8,128)S(1)}, f32[7,144,128]{2,1,0:T(8,128)}, u32[]{:S(2)}, u32[]{:S(2)}) %collective-permute-start.18) | collective-permute-done | bytes 516128 | tf_op jit(solution)/shard_map/cond/branch_18_fun/ppermute | solution.py:471
  40.0 8.8 %conditional.3 = (f32[7,144,128]{2,1,0:T(8,128)}) conditional(s32[]{:T(128)} %convert_element_type.3, f32[7,144,128]{2,1,0:T(8,128)} %get-tuple-element.102.first, f32[7,144,128]{2,1,0:T(8,128)} %get-tuple-element.102.first), branch_computations={%region_32.33_spmd, %region_33.34_spmd} | conditional | bytes 2064432 | solution.py:491
  40.0 8.8 %collective-permute-done.33 = f32[7,144,128]{2,1,0:T(8,128)} collective-permute-done((f32[7,144,128]{2,1,0:T(8,128)}, f32[7,144,128]{2,1,0:T(8,128)}, u32[]{:S(2)}, u32[]{:S(2)}) %collective-permute-start.33) | collective-permute-done | bytes 516128 | tf_op jit(solution)/shard_map/cond/branch_1_fun/ppermute | solution.py:492
  48.8 2.7 %select.15 = f32[4,7,96,128]{3,2,1,0:T(8,128)S(1)} custom-call(s32[1,2]{1,0:T(1,128)S(1)} %add_bitcast_fusion.offset, f32[7,144,128]{2,1,0:T(8,128)S(1)} %pad_maximum_fusion.ghosted, f32[7,144,128]{2,1,0:T(8,128)} %get-tuple-element.102.first, f32[7,144,128]{2,1,0:T(8,128)} %get-tuple-element.103.second), custom_call_target="tpu_custom_call" | custom-call | tf_op jit(solution)/shard_map/select/pallas_call | solution.py:495
  51.5 21.3 %all_to_all.54.recv = f32[4,7,96,128]{3,2,1,0:T(8,128)S(1)} all-to-all(f32[4,7,96,128]{3,2,1,0:T(8,128)S(1)} %select.15), channel_id=1, replica_groups=mesh['lat'=4,'x'=4,'z'=8,'core'=2] {'lat'}, dimensions={0} | all-to-all | bytes 2752512 | tf_op jit(solution)/shard_map/all_to_all | solution.py:502
  72.7 11.7 %phase_one.1 = (f32[9,64,8,128]{3,2,1,0:T(8,128)}, f32[4,72,8,128]{3,2,1,0:T(8,128)S(1)}, f32[16,8,128]{2,1,0:T(8,128)S(1)}, f32[16,8,128]{2,1,0:T(8,128)S(1)}, ...) custom-call(f32[4,7,96,128]{3,2,1,0:T(8,128)S(1)} %all_to_all.54.recv), custom_call_target="tpu_custom_call" | custom-call | tf_op jit(solution)/shard_map/phase_one/pallas_call | solution.py:503
  85.7 13.1 %all_to_all.55 = f32[32,1,128]{2,1,0:T(1,128)} all-to-all(f32[32,1,128]{2,1,0:T(1,128)S(1)} %bitcast.21), channel_id=1, replica_groups=mesh['lat'=4,'x'=4,'z'=8,'core'=2] {'lat','x','core'}, dimensions={0} | all-to-all | bytes 32768 | tf_op jit(solution)/shard_map/all_to_all | solution.py:464
  98.8 1.3 add_near.2
  100.2 11.3 %all_to_all.56 = f32[8,2,128]{2,1,0:T(2,128)S(1)} all-to-all(f32[8,2,128]{2,1,0:T(2,128)} %bitcast.24), channel_id=1, replica_groups=mesh['lat'=4,'x'=4,'z'=8,'core'=2] {'z'}, dimensions={0} | all-to-all | bytes 16384 | tf_op jit(solution)/shard_map/all_to_all | solution.py:466
  113.1 8.9 %phase_two.1 = (f32[64,8,128]{2,1,0:T(8,128)S(1)}, f32[8,128]{1,0:T(8,128)S(1)}, f32[4,64,8,128]{3,2,1,0:T(8,128)S(1)}, f32[4,64,8,128]{3,2,1,0:T(8,128)S(1)}, f32[32,128]{1,0:T(8,128)S(1)}) custom-call(f32[16,128]{1,0:T(8,128)S(1)} %bitcast.18, f32[9,64,8,128]{3,2,1,0:T(8,128)} %get-tuple-element.87.coef, f32[4,72,8,128]{3,2,1,0:T(8,128)S(1)} %get-tuple-element.88.lines, ...), custom_call_target="tpu_custom_call" | custom-call | tf_op jit(solution)/shard_map/phase_two/pallas_call | solution.py:521
  124.8 12.4 %all_to_all.57 = f32[32,1,128]{2,1,0:T(1,128)} all-to-all(f32[32,1,128]{2,1,0:T(1,128)S(1)} %bitcast.20), channel_id=1, replica_groups=mesh['lat'=4,'x'=4,'z'=8,'core'=2] {'lat','x','core'}, dimensions={0} | all-to-all | bytes 32768 | tf_op jit(solution)/shard_map/all_to_all | solution.py:464
  137.2 1.3 add_near.3
  138.5 9.8 %all_to_all.58 = f32[8,2,128]{2,1,0:T(2,128)S(1)} all-to-all(f32[8,2,128]{2,1,0:T(2,128)} %bitcast.25), channel_id=1, replica_groups=mesh['lat'=4,'x'=4,'z'=8,'core'=2] {'z'}, dimensions={0} | all-to-all | bytes 16384 | tf_op jit(solution)/shard_map/all_to_all | solution.py:466
  148.3 1.2 copy-done.1
  149.6 1.2 copy-done.3
  151.7 2.0 %combine.1 = f32[4,2,32,128]{3,2,1,0:T(8,128)S(1)} custom-call(f32[16,128]{1,0:T(8,128)S(1)} %bitcast.19, f32[8,128]{1,0:T(8,128)S(1)} %get-tuple-element.96.y1, f32[64,8,128]{2,1,0:T(8,128)S(1)} %copy-done.5, f32[4,64,8,128]{3,2,1,0:T(8,128)S(1)} %get-tuple-element.93.v1, f32[4,64,8,128]{3,2,1,0:T(8,128)S(1)} %get-tuple-element.94.w1, ...), custom_call_target="tpu_custom_call" | custom-call | tf_op jit(solution)/shard_map/combine/pallas_call | solution.py:535
  153.8 7.9 %all_to_all.59.recv = f32[4,2,32,128]{3,2,1,0:T(8,128)} all-to-all(f32[4,2,32,128]{3,2,1,0:T(8,128)S(1)} %combine.1), channel_id=1, replica_groups=mesh['lat'=4,'x'=4,'z'=8,'core'=2] {'lat'}, dimensions={0} | all-to-all | bytes 262144 | tf_op jit(solution)/shard_map/all_to_all | solution.py:542
  161.7 1.7 %unpack.1 = (f32[128,128]{1,0:T(8,128)}, f32[128,128]{1,0:T(8,128)}) custom-call(f32[4,2,32,128]{3,2,1,0:T(8,128)} %all_to_all.59.recv), custom_call_target="tpu_custom_call" | custom-call | tf_op jit(solution)/shard_map/unpack/pallas_call | solution.py:543
  (23 shorter events, 7.7 us)
Async XLA Ops:
  3.4 4.1 %collective-permute-start.34 = (f32[7,8,128]{2,1,0:T(8,128)S(1)}, f32[7,8,128]{2,1,0:T(8,128)S(1)}, u32[]{:S(2)}, u32[]{:S(2)}) collective-permute-start(f32[7,8,128]{2,1,0:T(8,128)S(1)} %get-tuple-element.100), channel_id=1, source_target_pairs={{0,1},{1,2},{2,3},{3,4},{4,5},{5,6},{6,7},{7,8},{8,9},{9,10},{10,1... | collective-permute-start | bytes 86024 | tf_op jit(solution)/shard_map/ppermute | solution.py:487
  6.4 3.3 %collective-permute-start.35 = (f32[7,8,128]{2,1,0:T(8,128)S(1)}, f32[7,8,128]{2,1,0:T(8,128)S(1)}, u32[]{:S(2)}, u32[]{:S(2)}) collective-permute-start(f32[7,8,128]{2,1,0:T(8,128)S(1)} %get-tuple-element.101), channel_id=1, source_target_pairs={{0,63},{1,0},{2,1},{3,2},{4,3},{5,4},{6,5},{7,6},{8,7},{9,8},{10,9... | collective-permute-start | bytes 86024 | tf_op jit(solution)/shard_map/ppermute | solution.py:488
  10.8 29.2 %collective-permute-start.18 = (f32[7,144,128]{2,1,0:T(8,128)S(1)}, f32[7,144,128]{2,1,0:T(8,128)}, u32[]{:S(2)}, u32[]{:S(2)}) collective-permute-start(f32[7,144,128]{2,1,0:T(8,128)S(1)} %param.18), channel_id=1, source_target_pairs={{0,36},{1,35},{2,34},{3,33},{4,32},{5,31},{6,30},{7,29},{8,28},{9,... | collective-permute-start | bytes 1548296 | tf_op jit(solution)/shard_map/cond/branch_18_fun/ppermute | solution.py:471
  40.0 8.8 %collective-permute-start.33 = (f32[7,144,128]{2,1,0:T(8,128)}, f32[7,144,128]{2,1,0:T(8,128)}, u32[]{:S(2)}, u32[]{:S(2)}) collective-permute-start(f32[7,144,128]{2,1,0:T(8,128)} %param.33), channel_id=1, source_target_pairs={{0,63},{1,0},{2,1},{3,2},{4,3},{5,4},{6,5},{7,6},{8,7},{9,8},{10,9... | collective-permute-start | bytes 1548296 | tf_op jit(solution)/shard_map/cond/branch_1_fun/ppermute | solution.py:492
  84.5 0.6 copy-start.6
  85.1 0.6 copy-start.8
  111.5 0.8 copy-start.7
  112.3 0.8 copy-start.9
  122.0 1.0 copy-start
  123.1 1.0 copy-start.2
  124.0 0.7 copy-start.4
  148.3 1.2 copy-start.1
  149.6 1.2 copy-start.3
  150.8 0.9 copy-start.5
